TPU v7x, 32 devices: a whole 2x2x4 slice. The times are simulated.
32 devices in a mesh: dp: 4 (over z), row: 2 (over x), col: 4 (over y, core).
Axes of the slice: x: 2, y: 2, z: 4, core: 2. Of those that a mesh axis runs over, the one named last changes fastest.
Arguments:
- block_input: bfloat16 [8192, 1536], P('dp', 'row'), may hold values from -16 to 16
- positions: int32 [8192], P('dp'), may hold values from 0 to 511, as said below
- attn_gain: float32 [1536], P('row'), may hold values from 0.5 to 1.5
- w_qkv: bfloat16 [1536, 3072], P('row', 'col'), may hold values from -1.04613624 to 1.04613624
- w_out: bfloat16 [1536, 1536], P('col', 'row'), may hold values from -1.25 to 1.25
- ffn_gain: float32 [1536], P('row'), may hold values from 0.5 to 1.5
- w_gate: bfloat16 [1536, 4096], P('row', 'col'), may hold values from -0.15625 to 0.15625
- w_up: bfloat16 [1536, 4096], P('row', 'col'), may hold values from -0.15625 to 0.15625
- w_down: bfloat16 [4096, 1536], P('col', 'row'), may hold values from -0.09375 to 0.09375
- out_grad: bfloat16 [8192, 1536], P('dp', 'row'), may hold values from -6 to 6
Outputs:
- block_output: bfloat16 [8192, 1536], P('dp', 'row')
- input_grad: bfloat16 [8192, 1536], P('dp', 'row')
- attn_gain_grad: float32 [1536], P('row')
- w_qkv_grad: float32 [1536, 3072], P('row', 'col')
- w_out_grad: float32 [1536, 1536], P('col', 'row')
- ffn_gain_grad: float32 [1536], P('row')
- w_gate_grad: float32 [1536, 4096], P('row', 'col')
- w_up_grad: float32 [1536, 4096], P('row', 'col')
- w_down_grad: float32 [4096, 1536], P('col', 'row')
Inputs may be any that keep to these rules, and one draw needn't show every extreme that they name: `positions`: each sequence of 512 tokens holds one to five packed documents; a token's position counts from the first token of its document; some sequence is a single document.
All inputs are finite; a program needn't handle non-finite values.
Results may differ from a plain program's by a relative error of at most 0.015.
Values may be sent and summed in bfloat16 or wider, within the bound.
A program may use at most 192 MiB of HBM per device.

v0:
```python
import jax
import jax.numpy as jnp
from jax import lax
from jax.sharding import PartitionSpec as P

D = 1536
H = 16
KV = 8
HD = 96
SEQ_LEN = 512
EPS = 1e-05
THETA = 100000.0


def rotate(values, cosine, sine, sign):
    half = values.shape[-1] // 2
    first = values[..., :half]
    second = values[..., half:]
    return jnp.concatenate(
        [first * cosine - sign * second * sine, second * cosine + sign * first * sine], axis=-1
    )


def angle_tables(pos):
    freqs = THETA ** (-(jnp.arange(0, HD, 2).astype(jnp.float32) / HD))
    angles = pos.astype(jnp.float32)[..., None] * freqs
    return (jnp.cos(angles), jnp.sin(angles))


def norm_stat(values):
    return lax.psum(values, "row")


def width_total(values):
    return lax.psum(values, "col")


def join_rows(values):
    return lax.all_gather(values, "row", axis=0, tiled=True)


def split_rows(left, right, contract):
    return lax.psum_scatter(
        lax.dot_general(
            left, right, (((1,), (contract,)), ((), ())), preferred_element_type=jnp.float32
        ),
        "row",
        scatter_dimension=0,
        tiled=True,
    )


def left_product(left, right):
    return lax.dot_general(
        left, right, (((0,), (0,)), ((), ())), preferred_element_type=jnp.float32
    )


def right_product(left, right):
    return lax.dot_general(
        left, right, (((1,), (1,)), ((), ())), preferred_element_type=jnp.float32
    )


def swiglu_back(gate, up, grad):
    sig = jax.nn.sigmoid(gate)
    gate_grad = (grad * up * sig * (1.0 + gate * (1.0 - sig))).astype(jnp.bfloat16)
    up_grad = (grad * gate * sig).astype(jnp.bfloat16)
    return (gate_grad, up_grad)


def body(block_input, positions, attn_gain, w_qkv, w_out, ffn_gain, w_gate, w_up, w_down, out_grad):
    f32 = jnp.float32
    bf = jnp.bfloat16
    rows_all = block_input.shape[0]
    rows_half = rows_all // lax.axis_size("row")
    group = H // KV
    kv_local = w_qkv.shape[1] // ((group + 2) * HD)
    seqs_local = rows_half // SEQ_LEN
    scale = HD ** (-0.5)
    xf = block_input.astype(f32)
    inv1 = lax.rsqrt(norm_stat(jnp.sum(xf * xf, axis=1, keepdims=True)) / D + EPS)
    normed1 = (xf * inv1 * attn_gain).astype(bf)
    qkv_half = split_rows(normed1, w_qkv, 0)
    grouped = qkv_half.reshape(seqs_local, SEQ_LEN, kv_local, group + 2, HD)
    pos_half = lax.dynamic_slice_in_dim(
        positions, lax.axis_index("row") * rows_half, rows_half
    ).reshape(seqs_local, SEQ_LEN)
    cosine, sine = angle_tables(pos_half)
    cq = cosine[:, :, None, None, :]
    sq = sine[:, :, None, None, :]
    ck = cosine[:, :, None, :]
    sk = sine[:, :, None, :]
    queries = rotate(grouped[:, :, :, :group], cq, sq, 1.0).astype(bf)
    keys = rotate(grouped[:, :, :, group], ck, sk, 1.0).astype(bf)
    vals = grouped[:, :, :, group + 1].astype(bf)
    causal = jnp.arange(SEQ_LEN)[:, None] >= jnp.arange(SEQ_LEN)[None, :]
    scores = jnp.einsum("sikph,sjkh->skpij", queries, keys, preferred_element_type=f32) * scale
    scores = jnp.where(causal, scores, -1e30)
    top = jnp.max(scores, axis=-1, keepdims=True)
    lse = top + jnp.log(jnp.sum(jnp.exp(scores - top), axis=-1, keepdims=True))
    probs_b = jnp.exp(scores - lse).astype(bf)
    mixed = jnp.einsum("skpij,sjkh->sikph", probs_b, vals, preferred_element_type=f32).astype(bf)
    attn_rows = join_rows(mixed.reshape(rows_half, kv_local * group * HD))
    hidden = xf + width_total(jnp.dot(attn_rows, w_out, preferred_element_type=f32))
    inv2 = lax.rsqrt(norm_stat(jnp.sum(hidden * hidden, axis=1, keepdims=True)) / D + EPS)
    normed2 = (hidden * inv2 * ffn_gain).astype(bf)
    gate_part = jnp.dot(normed2, w_gate, preferred_element_type=f32)
    up_part = jnp.dot(normed2, w_up, preferred_element_type=f32)
    gate_kept, up_kept = (
        lax.psum_scatter(gate_part, "row", scatter_dimension=0, tiled=True),
        lax.psum_scatter(up_part, "row", scatter_dimension=0, tiled=True),
    )
    act_half = (jax.nn.silu(gate_kept) * up_kept).astype(bf)
    act_rows = lax.all_gather(act_half, "row", axis=0, tiled=True)
    block_output = (
        hidden + width_total(jnp.dot(act_rows, w_down, preferred_element_type=f32))
    ).astype(bf)
    w_down_grad = left_product(act_rows, out_grad)
    act_grad_part = right_product(out_grad, w_down)
    act_grad_half = lax.psum_scatter(act_grad_part, "row", scatter_dimension=0, tiled=True)
    gate_half, up_half = swiglu_back(gate_kept, up_kept, act_grad_half)
    gate_grad, up_grad = (
        lax.all_gather(gate_half, "row", axis=0, tiled=True),
        lax.all_gather(up_half, "row", axis=0, tiled=True),
    )
    w_gate_grad = left_product(normed2, gate_grad)
    w_up_grad = left_product(normed2, up_grad)
    normed2_grad = width_total(right_product(gate_grad, w_gate) + right_product(up_grad, w_up))
    ffn_gain_grad = jnp.sum(normed2_grad * hidden * inv2, axis=0)
    scaled2 = normed2_grad * ffn_gain
    hidden_grad = out_grad.astype(f32) + inv2 * (
        scaled2
        - hidden * inv2 * inv2 * norm_stat(jnp.sum(scaled2 * hidden, axis=1, keepdims=True)) / D
    )
    hidden_b = hidden_grad.astype(bf)
    w_out_grad = left_product(attn_rows, hidden_b)
    mixed_grad = (
        split_rows(hidden_b, w_out, 1).astype(bf).reshape(seqs_local, SEQ_LEN, kv_local, group, HD)
    )
    probs = jnp.exp(scores - lse)
    value_grad = jnp.einsum("skpij,sikph->sjkh", probs_b, mixed_grad, preferred_element_type=f32)
    prob_grad = jnp.einsum("sikph,sjkh->skpij", mixed_grad, vals, preferred_element_type=f32)
    delta = jnp.sum(mixed_grad.astype(f32) * mixed.astype(f32), axis=-1)
    delta = jnp.transpose(delta, (0, 2, 3, 1))[..., None]
    score_grad = (probs * (prob_grad - delta)).astype(bf)
    query_grad = rotate(
        jnp.einsum("skpij,sjkh->sikph", score_grad, keys, preferred_element_type=f32) * scale,
        cq,
        sq,
        -1.0,
    )
    key_grad = rotate(
        jnp.einsum("skpij,sikph->sjkh", score_grad, queries, preferred_element_type=f32) * scale,
        ck,
        sk,
        -1.0,
    )
    packed = jnp.concatenate(
        [query_grad, key_grad[:, :, :, None], value_grad[:, :, :, None]], axis=3
    ).astype(bf)
    qkv_grad = join_rows(packed.reshape(rows_half, w_qkv.shape[1]))
    w_qkv_grad = left_product(normed1, qkv_grad)
    normed1_grad = width_total(right_product(qkv_grad, w_qkv))
    attn_gain_grad = jnp.sum(normed1_grad * xf * inv1, axis=0)
    scaled1 = normed1_grad * attn_gain
    input_grad = (
        hidden_grad
        + inv1
        * (scaled1 - xf * inv1 * inv1 * norm_stat(jnp.sum(scaled1 * xf, axis=1, keepdims=True)) / D)
    ).astype(bf)
    attn_gain_grad, w_qkv_grad, w_out_grad, ffn_gain_grad, w_gate_grad, w_up_grad, w_down_grad = (
        lax.psum(attn_gain_grad.astype(jnp.bfloat16), "dp").astype(jnp.float32),
        lax.psum(w_qkv_grad.astype(jnp.bfloat16), "dp").astype(jnp.float32),
        lax.psum(w_out_grad.astype(jnp.bfloat16), "dp").astype(jnp.float32),
        lax.psum(ffn_gain_grad.astype(jnp.bfloat16), "dp").astype(jnp.float32),
        lax.psum(w_gate_grad.astype(jnp.bfloat16), "dp").astype(jnp.float32),
        lax.psum(w_up_grad.astype(jnp.bfloat16), "dp").astype(jnp.float32),
        lax.psum(w_down_grad.astype(jnp.bfloat16), "dp").astype(jnp.float32),
    )
    return (
        block_output,
        input_grad,
        attn_gain_grad,
        w_qkv_grad,
        w_out_grad,
        ffn_gain_grad,
        w_gate_grad,
        w_up_grad,
        w_down_grad,
    )


def solution(mesh):
    return jax.shard_map(
        body,
        mesh=mesh,
        in_specs=(
            P("dp", "row"),
            P("dp"),
            P("row"),
            P("row", "col"),
            P("col", "row"),
            P("row"),
            P("row", "col"),
            P("row", "col"),
            P("col", "row"),
            P("dp", "row"),
        ),
        out_specs=(
            P("dp", "row"),
            P("dp", "row"),
            P("row"),
            P("row", "col"),
            P("col", "row"),
            P("row"),
            P("row", "col"),
            P("row", "col"),
            P("col", "row"),
        ),
        check_vma=False,
    )
```

profile of v0, /device:TPU:0, one launch (start us, length us, event | category | flops | bytes accessed | tf_op | source)
XLA Modules:
  0.0 1491.3 jit_solution(6194909048291860447)
XLA Ops:
  7.2 2.7 fusion.12
  9.9 5.9 psum.105
  15.9 7.6 fusion.30
  25.0 77.5 %reduce-scatter.6.cloned.1.call-done = f32[1024,768]{1,0:T(8,128)} async-done(((f32[2048,768]{1,0:T(8,128)}), f32[1024,768]{1,0:T(8,128)}) %reduce-scatter.6.cloned.1.call-update) | async-done | bytes 3145744 | tf_op jit(solution)/shard_map/reduce_scatter | solution.py:43
  102.6 3.5 copy.27
  106.1 5.6 reshape.64
  121.5 3.3 fusion.24
  126.9 27.1 %all-gather.6.cloned.1.call-done = bf16[2048,384]{0,1:T(8,128)(2,1)} async-done(((bf16[1024,384]{0,1:T(8,128)(2,1)}), bf16[2048,384]{0,1:T(8,128)(2,1)}) %all-gather.6.cloned.1.call-update) | async-done | bytes 1572880 | tf_op jit(solution)/shard_map/all_gather | solution.py:39
  154.0 6.0 fusion.42
  160.1 9.1 fusion.46
  169.3 110.5 %all-reduce.8.cloned.1.call-done = f32[2048,768]{1,0:T(8,128)} async-done(((f32[2048,768]{1,0:T(8,128)}), f32[2048,768]{1,0:T(8,128)}) %all-reduce.8.cloned.1.call-update) | async-done | bytes 6291472 | tf_op jit(solution)/shard_map/psum | solution.py:35
  279.8 7.2 multiply_reduce_fusion.2
  287.0 5.2 psum.107
  292.2 3.5 multiply_convert_fusion
  297.4 5.6 fusion.44
  303.1 7.6 fusion.43
  310.8 70.9 %reduce-scatter.12.cloned.1.call-done = f32[1024,1024]{1,0:T(8,128)} async-done(((f32[2048,1024]{1,0:T(8,128)}), f32[1024,1024]{1,0:T(8,128)}) %reduce-scatter.12.cloned.1.call-update) | async-done | bytes 4194320 | tf_op jit(solution)/shard_map/reduce_scatter | solution.py:121
  381.7 101.5 %reduce-scatter.10.cloned.1.call-done = f32[1024,1024]{1,0:T(8,128)} async-done(((f32[2048,1024]{1,0:T(8,128)}), f32[1024,1024]{1,0:T(8,128)}) %reduce-scatter.10.cloned.1.call-update) | async-done | bytes 4194320 | tf_op jit(solution)/shard_map/reduce_scatter | solution.py:112
  483.2 101.5 %reduce-scatter.8.cloned.1.call-done = f32[1024,1024]{1,0:T(8,128)} async-done(((f32[2048,1024]{1,0:T(8,128)}), f32[1024,1024]{1,0:T(8,128)}) %reduce-scatter.8.cloned.1.call-update) | async-done | bytes 4194320 | tf_op jit(solution)/shard_map/reduce_scatter | solution.py:111
  584.7 8.1 multiply_convert_fusion.1
  594.1 55.6 %all-gather.10.cloned.1.call-done = bf16[2048,1024]{1,0:T(8,128)(2,1)} async-done(((bf16[1024,1024]{1,0:T(8,128)(2,1)}), bf16[2048,1024]{1,0:T(8,128)(2,1)}) %all-gather.10.cloned.1.call-update) | async-done | bytes 4194320 | tf_op jit(solution)/shard_map/all_gather | solution.py:124
  649.7 8.3 fusion.47
  658.0 50.6 %all-gather.12.cloned.1.call-done = bf16[2048,1024]{1,0:T(8,128)(2,1)} async-done(((bf16[1024,1024]{1,0:T(8,128)(2,1)}), bf16[2048,1024]{1,0:T(8,128)(2,1)}) %all-gather.12.cloned.1.call-update) | async-done | bytes 4194320 | tf_op jit(solution)/shard_map/all_gather | solution.py:125
  708.6 10.6 convolution_add_fusion
  719.3 119.7 %all-reduce.10.cloned.1.call-done = f32[2048,768]{1,0:T(8,128)} async-done(((f32[2048,768]{1,0:T(8,128)}), f32[2048,768]{1,0:T(8,128)}) %all-reduce.10.cloned.1.call-update) | async-done | bytes 6291472 | tf_op jit(solution)/shard_map/psum | solution.py:35
  839.0 5.4 multiply_reduce_fusion
  844.4 5.0 psum.110
  849.4 6.7 multiply_add_fusion
  856.1 2.6 copy-done.2
  858.7 3.5 fusion.19
  863.2 42.8 %reduce-scatter.14.cloned.1.call-done = f32[1024,384]{1,0:T(8,128)} async-done(((f32[2048,384]{1,0:T(8,128)}), f32[1024,384]{1,0:T(8,128)}) %reduce-scatter.14.cloned.1.call-update) | async-done | bytes 1572880 | tf_op jit(solution)/shard_map/reduce_scatter | solution.py:43
  909.8 5.3 fusion.1
  925.8 39.1 %all-gather.8.cloned.1.call-done = bf16[2048,1024]{1,0:T(8,128)(2,1)} async-done(((bf16[1024,1024]{1,0:T(8,128)(2,1)}), bf16[2048,1024]{1,0:T(8,128)(2,1)}) %all-gather.8.cloned.1.call-update) | async-done | bytes 4194320 | tf_op jit(solution)/shard_map/all_gather | solution.py:115
  964.9 8.2 fusion.45
  973.1 38.7 %all-gather.14.cloned.1.call-done = bf16[2048,768]{0,1:T(8,128)(2,1)} async-done(((bf16[1024,768]{0,1:T(8,128)(2,1)}), bf16[2048,768]{0,1:T(8,128)(2,1)}) %all-gather.14.cloned.1.call-update) | async-done | bytes 3145744 | tf_op jit(solution)/shard_map/all_gather | solution.py:39
  1011.8 7.2 fusion.48
  1019.4 8.0 convolution_convert_fusion
  1027.3 4.6 convolution_convert_fusion.2
  1031.9 4.6 convolution_convert_fusion.1
  1039.6 4.2 convolution_convert_fusion.3
  1043.9 196.1 %all-reduce.12.cloned.1.call-done = (f32[2048,768]{1,0:T(8,128)}, f32[2048,768]{1,0:T(8,128)}) async-done(((f32[2048,768]{1,0:T(8,128)}, f32[2048,768]{1,0:T(8,128)}), (f32[2048,768]{1,0:T(8,128)}, f32[2048,768]{1,0:T(8,128)})) %all-reduce.12.cloned.1.call-update) | async-done | bytes 12582928 | tf_op jit(solution)/shard_map/psum | solution.py:35
  1239.9 4.9 fusion.15
  1244.8 12.2 all-reduce.1
  1258.2 5.2 psum.112
  1263.4 7.1 add_convert_fusion
  1273.8 3.2 fusion.11
  1277.0 196.2 %all-reduce.14.cloned.1.call-done = (bf16[768,768]{1,0:T(8,128)(2,1)}, bf16[384,768]{1,0:T(8,128)(2,1)}, bf16[768,1024]{1,0:T(8,128)(2,1)}, bf16[768,1024]{1,0:T(8,128)(2,1)}, bf16[1024,768]{1,0:T(8,128)(2,1)}) async-done(((bf16[768,768]{1,0:T(8,128)(2,1)}, bf16[384,768]{1,0:T(8,128)(2,1)}, bf16[768,1024]{1,0:T(8,128)(2,1)}, bf16[768,1024]{1,0:T(8,128)(2,1)}, bf16[1024,768]{1,0:T(8,128)(2,1)}), ...) | async-done | bytes 6488080 | tf_op jit(solution)/shard_map/psum | solution.py:174
  1473.3 3.0 convert_element_type.146
  (153 shorter events, 48.0 us)
Async XLA Ops:
  7.2 295.9 %copy-start = (bf16[768,1024]{1,0:T(8,128)(2,1)S(1)}, bf16[768,1024]{1,0:T(8,128)(2,1)}, u32[]{:S(2)}) copy-start(bf16[768,1024]{1,0:T(8,128)(2,1)} %param.16) | copy-start | bytes 4718596
  7.2 95.4 %reduce-scatter.6.cloned.1.call-start = ((), (), s32[]{:S(2)}) async-start(), calls=%async_computation.5 | async-start | bytes 9437184 | tf_op jit(solution)/shard_map/reduce_scatter | solution.py:43
  23.5 130.5 %all-gather.6.cloned.1.call-start = ((), (), s32[]{:S(2)}) async-start(), calls=%async_computation.6 | async-start | bytes 2359296 | tf_op jit(solution)/shard_map/all_gather | solution.py:39
  24.3 93.4 %copy-start.18 = (pred[512,512]{0,1:T(8,128)(4,1)}, pred[512,512]{0,1:T(8,128)(4,1)S(1)}, u32[]{:S(2)}) copy-start(pred[512,512]{0,1:T(8,128)(4,1)S(1)} %iota_compare_fusion) | copy-start | bytes 786436
  111.7 3.6 slice-start.4
  113.2 6.3 copy-start.24
  117.6 3.3 copy-start.6
  126.7 153.1 %all-reduce.8.cloned.1.call-start = ((), (), s32[]{:S(2)}) async-start(), calls=%async_computation.7 | async-start | bytes 12582912 | tf_op jit(solution)/shard_map/psum | solution.py:35
  160.1 221.6 %reduce-scatter.12.cloned.1.call-start = ((), (), s32[]{:S(2)}) async-start(), calls=%async_computation.11 | async-start | bytes 12582912 | tf_op jit(solution)/shard_map/reduce_scatter | solution.py:121
  169.3 122.9 %copy-start.25 = (f32[768]{0:T(1024)S(1)}, f32[768]{0:T(1024)}, u32[]{:S(2)}) copy-start(f32[768]{0:T(1024)} %param.15) | copy-start | bytes 9220
  169.3 313.9 %reduce-scatter.10.cloned.1.call-start = ((), (), s32[]{:S(2)}) async-start(), calls=%async_computation.9 | async-start | bytes 12582912 | tf_op jit(solution)/shard_map/reduce_scatter | solution.py:112
  292.2 5.2 copy-start.33
  303.0 281.6 %reduce-scatter.8.cloned.1.call-start = ((), (), s32[]{:S(2)}) async-start(), calls=%async_computation.8 | async-start | bytes 12582912 | tf_op jit(solution)/shard_map/reduce_scatter | solution.py:111
  310.7 339.0 %all-gather.10.cloned.1.call-start = ((), (), s32[]{:S(2)}) async-start(), calls=%async_computation.12 | async-start | bytes 6291456 | tf_op jit(solution)/shard_map/all_gather | solution.py:124
  592.8 115.8 %all-gather.12.cloned.1.call-start = ((), (), s32[]{:S(2)}) async-start(), calls=%async_computation.13 | async-start | bytes 6291456 | tf_op jit(solution)/shard_map/all_gather | solution.py:125
  593.6 245.4 %all-reduce.10.cloned.1.call-start = ((), (), s32[]{:S(2)}) async-start(), calls=%async_computation.14 | async-start | bytes 12582912 | tf_op jit(solution)/shard_map/psum | solution.py:35
  719.2 186.8 %reduce-scatter.14.cloned.1.call-start = ((), (), s32[]{:S(2)}) async-start(), calls=%async_computation.15 | async-start | bytes 4718592 | tf_op jit(solution)/shard_map/reduce_scatter | solution.py:43
  849.4 9.3 copy-start.10
  856.1 2.6 copy-start.2
  862.2 102.7 %all-gather.8.cloned.1.call-start = ((), (), s32[]{:S(2)}) async-start(), calls=%async_computation.10 | async-start | bytes 6291456 | tf_op jit(solution)/shard_map/all_gather | solution.py:115
  863.0 148.8 %all-gather.14.cloned.1.call-start = ((), (), s32[]{:S(2)}) async-start(), calls=%async_computation.16 | async-start | bytes 4718592 | tf_op jit(solution)/shard_map/all_gather | solution.py:39
  909.8 5.4 copy-start.15
  909.8 5.4 copy-start.17
  915.2 3.0 slice-start.5
  916.8 3.2 slice-start.6
  916.8 3.2 copy-start.19
  916.9 3.2 copy-start.28
  922.5 42.4 %copy-start.34 = (bf16[1024,768]{1,0:T(8,128)(2,1)S(1)}, bf16[1024,768]{1,0:T(8,128)(2,1)}, u32[]{:S(2)}) copy-start(bf16[1024,768]{1,0:T(8,128)(2,1)} %param.18) | copy-start | bytes 4718596
  925.8 86.1 %copy-start.35 = (bf16[768,768]{1,0:T(8,128)(2,1)S(1)}, bf16[768,768]{1,0:T(8,128)(2,1)}, u32[]{:S(2)}) copy-start(bf16[768,768]{1,0:T(8,128)(2,1)} %param.13) | copy-start | bytes 3538948
  925.8 314.2 %all-reduce.12.cloned.1.call-start = ((), (), s32[]{:S(2)}) async-start(), calls=%async_computation.17 | async-start | bytes 25165824 | tf_op jit(solution)/shard_map/psum | solution.py:35
  1019.1 454.2 %all-reduce.14.cloned.1.call-start = ((), (), s32[]{:S(2)}) async-start(), calls=%async_computation.18 | async-start | bytes 12976128 | tf_op jit(solution)/shard_map/psum | solution.py:174
  1019.3 8.0 copy-start.8
  1019.4 8.0 copy-start.30
  1027.3 4.6 copy-start.31
  1027.3 9.1 slice-start
  1031.9 4.6 slice-start.1
  1031.9 4.6 copy-start.9
  1036.5 2.3 copy-start.3
  1036.5 2.3 copy-start.26
  1036.5 3.1 copy-start.32
  1263.4 7.1 slice-start.2
  1263.4 7.1 slice-start.3
  1263.4 8.5 copy-start.4
  1263.4 10.4 copy-start.5
  1473.3 5.2 copy-start.13
  1473.3 7.2 copy-start.12
  1478.4 4.1 copy-start.11
  1480.5 4.0 copy-start.1
  (9 other events, 13.6 us)
Sparse Core Ops, SparseCore 0:
  23.6 78.9 reduce-scatter.5
  126.8 27.1 all-gather.5
  160.2 119.5 all-reduce.7
  282.0 99.6 reduce-scatter.11
  383.8 99.3 reduce-scatter.9
  485.3 99.2 reduce-scatter.7
  593.0 56.7 all-gather.9
  651.9 56.7 all-gather.11
  719.4 119.5 all-reduce.9
  862.4 43.6 reduce-scatter.13
  908.1 56.7 all-gather.7
  966.9 44.8 all-gather.13
  1019.2 220.6 all-reduce.11
  1243.7 229.5 all-reduce.13
where the time goes:
time: 1490 us
  waiting for transfers between devices  1230 us (83%)
  matrix products  112 us (8%)
  other arithmetic  66.5 us (4%)
  blocking collectives  33.5 us (2%)
  local copies, waits for them, and re-layouts  33.1 us (2%)
    psum x3, waiting for transfers between devices, width_total(): return lax.psum(values, 'col')  426 us
    psum x1, waiting for transfers between devices, body(): lax.psum(w_qkv_grad.astype(jnp.bfloat16), 'dp').astype(jnp.float32)  196 us
    reduce_scatter x2, waiting for transfers between devices, split_rows(): lax.psum_scatter(lax.dot_general(left, right, (((1,), (contract,)), ((),...  120 us
    reduce_scatter x1, waiting for transfers between devices, body(): lax.psum_scatter(up_part, 'row', scatter_dimension=0, tiled=True)  102 us
    reduce_scatter x1, waiting for transfers between devices, body(): lax.psum_scatter(gate_part, 'row', scatter_dimension=0, tiled=True)  101 us
    reduce_scatter x1, waiting for transfers between devices, body(): lax.psum_scatter(act_grad_part, 'row', scatter_dimension=0, tiled=True)  70.9 us
    all_gather x2, waiting for transfers between devices, join_rows(): return lax.all_gather(values, 'row', axis=0, tiled=True)  65.8 us
    all_gather x1, waiting for transfers between devices, body(): lax.all_gather(gate_half, 'row', axis=0, tiled=True)  55.6 us
  transfers between devices with their start and end apart: 14, of which 14 were waited for; matrix products, arithmetic and copies ran while one was open for 7% of the time, Pallas kernels for 0%

commit v1 on v0

--- a/solution.py
+++ b/solution.py
@@ -32,7 +32,7 @@
 
 
 def width_total(values):
-    return lax.psum(values, "col")
+    return jnp.sum(lax.all_gather(values, "col"), axis=0)
 
 
 def join_rows(values):

time: 1490 us -> 1700 us (1.14)
  waiting for transfers between devices: 1230 us -> 1370 us
  other arithmetic: 66.5 us -> 126 us
    all_gather x0 -> x4, waiting for transfers between devices: none -> 562 us  [width_total(): return jnp.sum(lax.all_gather(values, 'col'), axis=0)]
    psum x3 -> x0, waiting for transfers between devices: 426 us -> none  [width_total(): return lax.psum(values, 'col')]
    reduce_sum x0 -> x4, other arithmetic: none -> 53.6 us  [width_total(): return jnp.sum(lax.all_gather(values, 'col'), axis=0)]
    psum x1, waiting for transfers between devices: 196 us -> 221 us  [body(): lax.psum(w_qkv_grad.astype(jnp.bfloat16), 'dp').astype(jnp.float32)]
  transfers between devices with their start and end apart: 14 -> 15, of which waited for: 14 -> 15; matrix products, arithmetic and copies ran while one was open for 7% -> 8% of each run, Pallas kernels for 0% -> 0%
where the time goes in v1:
time: 1700 us
  waiting for transfers between devices  1370 us (81%)
  other arithmetic  126 us (7%)
  matrix products  121 us (7%)
  blocking collectives  32.8 us (2%)
  local copies, waits for them, and re-layouts  27.7 us (2%)
    all_gather x4, waiting for transfers between devices, width_total(): return jnp.sum(lax.all_gather(values, 'col'), axis=0)  562 us
    psum x1, waiting for transfers between devices, body(): lax.psum(w_qkv_grad.astype(jnp.bfloat16), 'dp').astype(jnp.float32)  221 us
    reduce_scatter x2, waiting for transfers between devices, split_rows(): lax.psum_scatter(lax.dot_general(left, right, (((1,), (contract,)), ((),...  121 us
    reduce_scatter x1, waiting for transfers between devices, body(): lax.psum_scatter(gate_part, 'row', scatter_dimension=0, tiled=True)  102 us
    reduce_scatter x1, waiting for transfers between devices, body(): lax.psum_scatter(up_part, 'row', scatter_dimension=0, tiled=True)  102 us
    reduce_scatter x1, waiting for transfers between devices, body(): lax.psum_scatter(act_grad_part, 'row', scatter_dimension=0, tiled=True)  57 us
    all_gather x1, waiting for transfers between devices, body(): lax.all_gather(gate_half, 'row', axis=0, tiled=True)  55.3 us
    reduce_sum x4, other arithmetic, width_total(): return jnp.sum(lax.all_gather(values, 'col'), axis=0)  53.6 us
  transfers between devices with their start and end apart: 15, of which 15 were waited for; matrix products, arithmetic and copies ran while one was open for 8% of the time, Pallas kernels for 0%

profile of v1, /device:TPU:0, one launch (start us, length us, event | category | flops | bytes accessed | tf_op | source)
XLA Modules:
  0.0 1696.0 jit_solution(13305660452156233386)
XLA Ops:
  9.9 5.9 psum.77
  16.5 7.6 fusion.30
  25.6 77.5 %reduce-scatter.6.cloned.1.call-done = f32[1024,768]{1,0:T(8,128)} async-done(((f32[2048,768]{1,0:T(8,128)}), f32[1024,768]{1,0:T(8,128)}) %reduce-scatter.6.cloned.1.call-update) | async-done | bytes 3145744 | tf_op jit(solution)/shard_map/reduce_scatter | solution.py:43
  103.2 3.5 copy.27
  106.7 5.6 reshape.64
  127.0 27.0 %all-gather.14.cloned.1.call-done = bf16[2048,384]{0,1:T(8,128)(2,1)} async-done(((bf16[1024,384]{0,1:T(8,128)(2,1)}), bf16[2048,384]{0,1:T(8,128)(2,1)}) %all-gather.14.cloned.1.call-update) | async-done | bytes 1572880 | tf_op jit(solution)/shard_map/all_gather | solution.py:39
  154.0 6.0 fusion.42
  160.1 11.0 fusion.46
  171.1 143.8 %all-gather.24.cloned.1.call-done = f32[8192,768]{1,0:T(8,128)} async-done(((f32[2048,768]{1,0:T(8,128)}), f32[8192,768]{1,0:T(8,128)}) %all-gather.24.cloned.1.call-update) | async-done | bytes 25165840 | tf_op jit(solution)/shard_map/all_gather | solution.py:35
  315.0 13.3 reduce_sum.110
  328.3 7.2 multiply_reduce_fusion.2
  335.4 5.3 psum.78
  345.9 5.6 fusion.44
  351.6 7.6 fusion.43
  359.7 57.0 %reduce-scatter.12.cloned.1.call-done = f32[1024,1024]{1,0:T(8,128)} async-done(((f32[2048,1024]{1,0:T(8,128)}), f32[1024,1024]{1,0:T(8,128)}) %reduce-scatter.12.cloned.1.call-update) | async-done | bytes 4194320 | tf_op jit(solution)/shard_map/reduce_scatter | solution.py:121
  416.7 101.5 %reduce-scatter.10.cloned.1.call-done = f32[1024,1024]{1,0:T(8,128)} async-done(((f32[2048,1024]{1,0:T(8,128)}), f32[1024,1024]{1,0:T(8,128)}) %reduce-scatter.10.cloned.1.call-update) | async-done | bytes 4194320 | tf_op jit(solution)/shard_map/reduce_scatter | solution.py:112
  518.2 101.5 %reduce-scatter.8.cloned.1.call-done = f32[1024,1024]{1,0:T(8,128)} async-done(((f32[2048,1024]{1,0:T(8,128)}), f32[1024,1024]{1,0:T(8,128)}) %reduce-scatter.8.cloned.1.call-update) | async-done | bytes 4194320 | tf_op jit(solution)/shard_map/reduce_scatter | solution.py:111
  619.7 8.1 multiply_convert_fusion.1
  629.4 55.3 %all-gather.18.cloned.1.call-done = bf16[2048,1024]{1,0:T(8,128)(2,1)} async-done(((bf16[1024,1024]{1,0:T(8,128)(2,1)}), bf16[2048,1024]{1,0:T(8,128)(2,1)}) %all-gather.18.cloned.1.call-update) | async-done | bytes 4194320 | tf_op jit(solution)/shard_map/all_gather | solution.py:124
  684.7 8.3 fusion.47
  693.1 50.5 %all-gather.20.cloned.1.call-done = bf16[2048,1024]{1,0:T(8,128)(2,1)} async-done(((bf16[1024,1024]{1,0:T(8,128)(2,1)}), bf16[2048,1024]{1,0:T(8,128)(2,1)}) %all-gather.20.cloned.1.call-update) | async-done | bytes 4194320 | tf_op jit(solution)/shard_map/all_gather | solution.py:125
  743.6 11.0 convolution_add_fusion
  754.9 47.6 %all-gather.16.cloned.1.call-done = bf16[2048,1024]{1,0:T(8,128)(2,1)} async-done(((bf16[1024,1024]{1,0:T(8,128)(2,1)}), bf16[2048,1024]{1,0:T(8,128)(2,1)}) %all-gather.16.cloned.1.call-update) | async-done | bytes 4194320 | tf_op jit(solution)/shard_map/all_gather | solution.py:115
  802.5 8.7 fusion.45
  811.3 147.5 %all-gather.28.cloned.1.call-done = f32[8192,768]{1,0:T(8,128)} async-done(((f32[2048,768]{1,0:T(8,128)}), f32[8192,768]{1,0:T(8,128)}) %all-gather.28.cloned.1.call-update) | async-done | bytes 25165840 | tf_op jit(solution)/shard_map/all_gather | solution.py:35
  958.7 14.9 reduce_sum.113
  973.6 8.7 multiply_reduce_fusion
  982.3 5.0 psum.79
  987.3 127.9 %all-gather.26.cloned.1.call-done = f32[8192,768]{1,0:T(8,128)} async-done(((f32[2048,768]{1,0:T(8,128)}), f32[8192,768]{1,0:T(8,128)}) %all-gather.26.cloned.1.call-update) | async-done | bytes 25165840 | tf_op jit(solution)/shard_map/all_gather | solution.py:35
  1115.1 12.7 reduce_sum.112
  1127.8 10.2 multiply_add_fusion
  1140.7 3.5 fusion.19
  1144.6 43.3 %reduce-scatter.14.cloned.1.call-done = f32[1024,384]{1,0:T(8,128)} async-done(((f32[2048,384]{1,0:T(8,128)}), f32[1024,384]{1,0:T(8,128)}) %reduce-scatter.14.cloned.1.call-update) | async-done | bytes 1572880 | tf_op jit(solution)/shard_map/reduce_scatter | solution.py:43
  1191.7 5.6 fusion.28
  1197.4 5.2 fusion.1
  1209.0 8.0 convolution_convert_fusion
  1217.0 4.6 convolution_convert_fusion.2
  1221.6 4.6 convolution_convert_fusion.1
  1228.4 25.3 %all-gather.22.cloned.1.call-done = bf16[2048,768]{0,1:T(8,128)(2,1)} async-done(((bf16[1024,768]{0,1:T(8,128)(2,1)}), bf16[2048,768]{0,1:T(8,128)(2,1)}) %all-gather.22.cloned.1.call-update) | async-done | bytes 3145744 | tf_op jit(solution)/shard_map/all_gather | solution.py:39
  1253.8 6.9 convolution_convert_fusion.3
  1261.9 7.3 fusion.48
  1269.3 220.8 %all-reduce.4.cloned.1.call-done = (bf16[768,768]{1,0:T(8,128)(2,1)}, bf16[384,768]{1,0:T(8,128)(2,1)}, bf16[768,1024]{1,0:T(8,128)(2,1)}, bf16[768,1024]{1,0:T(8,128)(2,1)}, bf16[1024,768]{1,0:T(8,128)(2,1)}) async-done(((bf16[768,768]{1,0:T(8,128)(2,1)}, bf16[384,768]{1,0:T(8,128)(2,1)}, bf16[768,1024]{1,0:T(8,128)(2,1)}, bf16[768,1024]{1,0:T(8,128)(2,1)}, bf16[1024,768]{1,0:T(8,128)(2,1)}), ...) | async-done | bytes 6488080 | tf_op jit(solution)/shard_map/psum | solution.py:174
  1501.9 143.3 %all-gather.30.cloned.1.call-done = f32[8192,768]{1,0:T(8,128)} async-done(((f32[2048,768]{1,0:T(8,128)}), f32[8192,768]{1,0:T(8,128)}) %all-gather.30.cloned.1.call-update) | async-done | bytes 25165840 | tf_op jit(solution)/shard_map/all_gather | solution.py:35
  1645.2 12.7 reduce_sum.116
  1657.9 4.9 fusion.15
  1662.8 11.7 all-reduce
  1675.7 5.0 psum.80
  1680.7 8.3 fusion.11
  (145 shorter events, 56.8 us)
Async XLA Ops:
  7.2 344.4 %copy-start = (bf16[768,1024]{1,0:T(8,128)(2,1)S(1)}, bf16[768,1024]{1,0:T(8,128)(2,1)}, u32[]{:S(2)}) copy-start(bf16[768,1024]{1,0:T(8,128)(2,1)} %param.16) | copy-start | bytes 4718596
  7.2 96.0 %reduce-scatter.6.cloned.1.call-start = ((), (), s32[]{:S(2)}) async-start(), calls=%async_computation.5 | async-start | bytes 9437184 | tf_op jit(solution)/shard_map/reduce_scatter | solution.py:43
  24.1 129.9 %all-gather.14.cloned.1.call-start = ((), (), s32[]{:S(2)}) async-start(), calls=%async_computation.6 | async-start | bytes 2359296 | tf_op jit(solution)/shard_map/all_gather | solution.py:39
  24.9 93.4 %copy-start.15 = (pred[512,512]{0,1:T(8,128)(4,1)}, pred[512,512]{0,1:T(8,128)(4,1)S(1)}, u32[]{:S(2)}) copy-start(pred[512,512]{0,1:T(8,128)(4,1)S(1)} %iota_compare_fusion) | copy-start | bytes 786436
  112.3 3.6 slice-start.2
  113.8 6.3 copy-start.21
  116.2 2.0 copy-start.17
  116.2 2.0 copy-start.19
  116.5 1.7 copy-start.11
  116.5 1.7 copy-start.13
  118.2 3.3 copy-start.3
  126.7 188.3 %all-gather.24.cloned.1.call-start = ((), (), s32[]{:S(2)}) async-start(), calls=%async_computation.15 | async-start | bytes 31457280 | tf_op jit(solution)/shard_map/all_gather | solution.py:35
  160.0 256.6 %reduce-scatter.12.cloned.1.call-start = ((), (), s32[]{:S(2)}) async-start(), calls=%async_computation.10 | async-start | bytes 12582912 | tf_op jit(solution)/shard_map/reduce_scatter | solution.py:121
  171.1 347.1 %reduce-scatter.10.cloned.1.call-start = ((), (), s32[]{:S(2)}) async-start(), calls=%async_computation.8 | async-start | bytes 12582912 | tf_op jit(solution)/shard_map/reduce_scatter | solution.py:112
  328.3 12.4 copy-start.25
  340.7 5.2 copy-start.31
  344.2 1.7 copy-start.4
  351.5 268.2 %reduce-scatter.8.cloned.1.call-start = ((), (), s32[]{:S(2)}) async-start(), calls=%async_computation.7 | async-start | bytes 12582912 | tf_op jit(solution)/shard_map/reduce_scatter | solution.py:111
  359.2 325.6 %all-gather.18.cloned.1.call-start = ((), (), s32[]{:S(2)}) async-start(), calls=%async_computation.11 | async-start | bytes 6291456 | tf_op jit(solution)/shard_map/all_gather | solution.py:124
  627.8 115.8 %all-gather.20.cloned.1.call-start = ((), (), s32[]{:S(2)}) async-start(), calls=%async_computation.12 | async-start | bytes 6291456 | tf_op jit(solution)/shard_map/all_gather | solution.py:125
  628.6 173.9 %all-gather.16.cloned.1.call-start = ((), (), s32[]{:S(2)}) async-start(), calls=%async_computation.9 | async-start | bytes 6291456 | tf_op jit(solution)/shard_map/all_gather | solution.py:115
  629.3 329.4 %all-gather.28.cloned.1.call-start = ((), (), s32[]{:S(2)}) async-start(), calls=%async_computation.17 | async-start | bytes 31457280 | tf_op jit(solution)/shard_map/all_gather | solution.py:35
  754.6 47.9 %copy-start.32 = (bf16[1024,768]{1,0:T(8,128)(2,1)S(1)}, bf16[1024,768]{1,0:T(8,128)(2,1)}, u32[]{:S(2)}) copy-start(bf16[1024,768]{1,0:T(8,128)(2,1)} %param.18) | copy-start | bytes 4718596
  754.6 360.5 %all-gather.26.cloned.1.call-start = ((), (), s32[]{:S(2)}) async-start(), calls=%async_computation.16 | async-start | bytes 31457280 | tf_op jit(solution)/shard_map/all_gather | solution.py:35
  811.2 376.6 %reduce-scatter.14.cloned.1.call-start = ((), (), s32[]{:S(2)}) async-start(), calls=%async_computation.13 | async-start | bytes 4718592 | tf_op jit(solution)/shard_map/reduce_scatter | solution.py:43
  1127.8 12.9 copy-start.7
  1138.0 2.7 copy-start.2
  1144.3 47.4 %copy-start.16 = (pred[512,512]{0,1:T(8,128)(4,1)S(1)}, pred[512,512]{0,1:T(8,128)(4,1)}, u32[]{:S(2)}) copy-start(pred[512,512]{0,1:T(8,128)(4,1)} %copy-done.15) | copy-start | bytes 786436
  1144.3 109.5 %all-gather.22.cloned.1.call-start = ((), (), s32[]{:S(2)}) async-start(), calls=%async_computation.14 | async-start | bytes 4718592 | tf_op jit(solution)/shard_map/all_gather | solution.py:39
  1191.7 5.7 copy-start.22
  1197.3 5.2 copy-start.12
  1197.4 5.2 copy-start.14
  1202.6 1.4 copy-start.18
  1208.7 281.4 %all-reduce.4.cloned.1.call-start = ((), (), s32[]{:S(2)}) async-start(), calls=%async_computation.19 | async-start | bytes 12976128 | tf_op jit(solution)/shard_map/psum | solution.py:174
  1209.0 8.0 copy-start.5
  1209.0 8.0 copy-start.29
  1217.0 4.6 copy-start.30
  1217.0 9.1 slice-start
  1221.6 4.6 slice-start.1
  1221.6 4.6 copy-start.6
  1226.1 27.6 %copy-start.24 = (f32[2048,1]{0,1:T(1,128)S(1)}, f32[2048,1]{0,1:T(1,128)}, u32[]{:S(2)}) copy-start(f32[2048,1]{0,1:T(1,128)} %copy-done.23) | copy-start | bytes 24580
  1226.1 27.6 %copy-start.26 = (f32[768]{0:T(1024)S(1)}, f32[768]{0:T(1024)}, u32[]{:S(2)}) copy-start(f32[768]{0:T(1024)} %param.12) | copy-start | bytes 9220
  1260.7 384.5 %all-gather.30.cloned.1.call-start = ((), (), s32[]{:S(2)}) async-start(), calls=%async_computation.18 | async-start | bytes 31457280 | tf_op jit(solution)/shard_map/all_gather | solution.py:35
  1490.1 5.2 copy-start.10
  1490.1 7.3 copy-start.9
  1495.3 4.5 copy-start.8
  1657.9 4.9 copy-start.27
  1680.7 8.3 copy-start.1
  (4 other events, 4.0 us)
Sparse Core Ops, SparseCore 0:
  24.2 78.9 reduce-scatter.5
  126.8 27.1 all-gather.13
  160.2 154.7 all-gather.23
  317.1 99.4 reduce-scatter.11
  418.8 99.3 reduce-scatter.9
  520.3 99.3 reduce-scatter.7
  628.0 56.7 all-gather.17
  686.8 56.7 all-gather.19
  745.7 56.7 all-gather.15
  803.9 154.7 all-gather.27
  960.3 154.7 all-gather.25
  1144.4 43.3 reduce-scatter.13
  1208.8 44.9 all-gather.21
  1260.8 229.2 all-reduce.3
  1491.5 153.6 all-gather.29
